TPU v7x, 32 devices: a whole 2x2x4 slice. The times are simulated.
32 devices in a mesh: dp: 2 (over x), sp: 4 (over z), tp: 4 (over y, core).
Axes of the slice: x: 2, y: 2, z: 4, core: 2. Of those that a mesh axis runs over, the one named last changes fastest.
Arguments:
- hidden: bfloat16 [128, 4096], P('dp'), parts along dimension 0
- new_pos: int32 [128], P('dp'), parts along dimension 0
- k_self: bfloat16 [128, 256, 8, 128], P('dp', 'sp', 'tp'), parts along dimension 0
- v_self: bfloat16 [128, 256, 8, 128], P('dp', 'sp', 'tp'), parts along dimension 0
- k_cross: bfloat16 [128, 256, 8, 128], P('dp', None, 'tp'), parts along dimension 0
- v_cross: bfloat16 [128, 256, 8, 128], P('dp', None, 'tp'), parts along dimension 0
- xvalid: int32 [128, 256], P('dp'), parts along dimension 0
- rowmask: int32 [128], P('dp'), parts along dimension 0
- self_attn_norm: bfloat16 [4096], replicated
- self_wq: bfloat16 [4096, 4096], P(None, 'tp')
- self_wk: bfloat16 [4096, 1024], P(None, 'tp')
- self_wv: bfloat16 [4096, 1024], P(None, 'tp')
- self_wo: bfloat16 [4096, 4096], P('tp')
- self_mlp_norm: bfloat16 [4096], replicated
- self_wgate: bfloat16 [4096, 14336], P(None, 'tp')
- self_wup: bfloat16 [4096, 14336], P(None, 'tp')
- self_wdown: bfloat16 [14336, 4096], P('tp')
- cross_attn_norm: bfloat16 [4096], replicated
- cross_wq: bfloat16 [4096, 4096], P(None, 'tp')
- cross_qnorm: bfloat16 [128], replicated
- cross_wo: bfloat16 [4096, 4096], P('tp')
- cross_gates: float32 [2], replicated
- cross_mlp_norm: bfloat16 [4096], replicated
- cross_wgate: bfloat16 [4096, 14336], P(None, 'tp')
- cross_wup: bfloat16 [4096, 14336], P(None, 'tp')
- cross_wdown: bfloat16 [14336, 4096], P('tp')
Outputs:
- output 1: bfloat16 [128, 4096], P('dp'), parts along dimension 0
- output 2: bfloat16 [128, 256, 8, 128], P('dp', 'sp', 'tp'), parts along dimension 0
- output 3: bfloat16 [128, 256, 8, 128], P('dp', 'sp', 'tp'), parts along dimension 0
There are 2 independent parts. A program takes and returns all parts, laid end to end along the dimension named above; an argument that names none is the same for every part.
All inputs are finite; a program needn't handle non-finite values.
Results may differ from a plain program's by a relative error of at most 0.0150412.
Values sent between devices are 32-bit elements.
A program may use at most 1 GiB of HBM per device.

v0:
```python
import math
import jax
import jax.numpy as jnp
from jax import lax
from jax.sharding import PartitionSpec as P

NORM_EPS = 1e-5
ROPE_THETA = 500000.0
ROPE_FACTOR = 8.0
LOW_FREQ = 1.0
HIGH_FREQ = 4.0
ORIG_CTX = 8192.0
NEG_BIG = -1e30


def rope_freqs(head_dim):
    inv_freq = 1.0 / (ROPE_THETA ** (jnp.arange(0, head_dim, 2).astype(jnp.float32) / head_dim))
    wavelen = 2.0 * math.pi / inv_freq
    smooth = (ORIG_CTX / wavelen - LOW_FREQ) / (HIGH_FREQ - LOW_FREQ)
    mid_freq = (1.0 - smooth) * inv_freq / ROPE_FACTOR + smooth * inv_freq
    scaled = jnp.where(wavelen > ORIG_CTX / LOW_FREQ, inv_freq / ROPE_FACTOR, mid_freq)
    return jnp.where(wavelen < ORIG_CTX / HIGH_FREQ, inv_freq, scaled)


def apply_rope(vectors, positions):
    head_dim = vectors.shape[-1]
    half_dim = head_dim // 2
    angles = positions.astype(jnp.float32)[:, None] * rope_freqs(head_dim)[None, :]
    cos_t = jnp.cos(angles)[:, None, :]
    sin_t = jnp.sin(angles)[:, None, :]
    first_half = vectors[..., :half_dim]
    second_half = vectors[..., half_dim:]
    return jnp.concatenate([first_half * cos_t - second_half * sin_t, second_half * cos_t + first_half * sin_t], axis=-1)


def rms_norm(values, gain_vec):
    vals32 = values.astype(jnp.float32)
    inv_rms = lax.rsqrt(jnp.mean(vals32 * vals32, axis=-1, keepdims=True) + NORM_EPS)
    return (vals32 * inv_rms * gain_vec.astype(jnp.float32)).astype(jnp.bfloat16)


def mlp_partial(normed, w_gate, w_up, w_down):
    gate_val = jnp.dot(normed, w_gate, preferred_element_type=jnp.float32).astype(jnp.bfloat16)
    up_val = jnp.dot(normed, w_up, preferred_element_type=jnp.float32).astype(jnp.bfloat16)
    hidden_act = (jax.nn.silu(gate_val.astype(jnp.float32)) * up_val.astype(jnp.float32)).astype(jnp.bfloat16)
    return jnp.dot(hidden_act, w_down, preferred_element_type=jnp.float32)


def local_softmax(queries, key_rows, val_rows, valid_mask, score_scale):
    scores = jnp.einsum('bkgd,btkd->bkgt', queries, key_rows, preferred_element_type=jnp.float32) * score_scale
    scores = jnp.where(valid_mask, scores, NEG_BIG)
    part_max = jnp.max(scores, axis=-1)
    probs_loc = jnp.where(valid_mask, jnp.exp(scores - part_max[..., None]), 0.0)
    part_sum = jnp.sum(probs_loc, axis=-1)
    part_out = jnp.einsum('bkgt,btkd->bkgd', probs_loc.astype(jnp.bfloat16), val_rows, preferred_element_type=jnp.float32)
    return part_max, part_sum, part_out


def combine_sp(part_max, part_sum, part_out):
    glob_max = lax.pmax(part_max, 'sp')
    factor = jnp.exp(part_max - glob_max)
    total_sum = lax.psum(part_sum * factor, 'sp')
    total_out = lax.psum(part_out * factor[..., None], 'sp')
    return total_out / total_sum[..., None]


def solution(mesh):
    cache_spec = P('dp', 'sp', 'tp', None)
    cross_spec = P('dp', None, 'tp', None)
    row_spec = P('dp', None)
    vec_spec = P('dp')
    full_spec = P(None)
    col_spec = P(None, 'tp')
    split_rows = P('tp', None)
    in_specs = (row_spec, vec_spec, cache_spec, cache_spec, cross_spec, cross_spec, row_spec, vec_spec,
                full_spec, col_spec, col_spec, col_spec, split_rows, full_spec, col_spec, col_spec, split_rows,
                full_spec, col_spec, full_spec, split_rows, full_spec, full_spec, col_spec, col_spec, split_rows)
    out_specs = (row_spec, cache_spec, cache_spec)

    def local_step(hidden, new_pos, k_self, v_self, k_cross, v_cross, xvalid, rowmask,
                   self_attn_norm, self_wq, self_wk, self_wv, self_wo, self_mlp_norm,
                   self_wgate, self_wup, self_wdown, cross_attn_norm, cross_wq, cross_qnorm,
                   cross_wo, cross_gates, cross_mlp_norm, cross_wgate, cross_wup, cross_wdown):
        batch_rows = hidden.shape[0]
        len_local = k_self.shape[1]
        kv_local = k_self.shape[2]
        head_dim = k_self.shape[3]
        heads_local = self_wq.shape[1] // head_dim
        group_size = heads_local // kv_local
        score_scale = head_dim ** -0.5
        normed = rms_norm(hidden, self_attn_norm)
        queries = jnp.dot(normed, self_wq, preferred_element_type=jnp.float32).astype(jnp.bfloat16)
        key_new = jnp.dot(normed, self_wk, preferred_element_type=jnp.float32).astype(jnp.bfloat16)
        val_new = jnp.dot(normed, self_wv, preferred_element_type=jnp.float32).astype(jnp.bfloat16)
        queries = apply_rope(queries.reshape(batch_rows, heads_local, head_dim).astype(jnp.float32), new_pos).astype(jnp.bfloat16)
        key_new = apply_rope(key_new.reshape(batch_rows, kv_local, head_dim).astype(jnp.float32), new_pos).astype(jnp.bfloat16)
        val_new = val_new.reshape(batch_rows, kv_local, head_dim)
        local_pos = new_pos - lax.axis_index('sp') * len_local
        slot_ids = jnp.arange(len_local)
        hit_mask = (slot_ids[None, :] == local_pos[:, None])[:, :, None, None]
        k_new_cache = jnp.where(hit_mask, key_new[:, None], k_self)
        v_new_cache = jnp.where(hit_mask, val_new[:, None], v_self)
        seen_mask = (slot_ids[None, :] <= local_pos[:, None])[:, None, None, :]
        self_stats = local_softmax(queries.reshape(batch_rows, kv_local, group_size, head_dim), k_new_cache, v_new_cache, seen_mask, score_scale)
        self_attn = combine_sp(self_stats[0], self_stats[1], self_stats[2])
        self_flat = self_attn.astype(jnp.bfloat16).reshape(batch_rows, heads_local * head_dim)
        attn_sum = lax.psum(jnp.dot(self_flat, self_wo, preferred_element_type=jnp.float32), 'tp')
        after_attn = (hidden.astype(jnp.float32) + attn_sum).astype(jnp.bfloat16)
        mlp_sum = lax.psum(mlp_partial(rms_norm(after_attn, self_mlp_norm), self_wgate, self_wup, self_wdown), 'tp')
        after_mlp = (after_attn.astype(jnp.float32) + mlp_sum).astype(jnp.bfloat16)
        normed = rms_norm(after_mlp, cross_attn_norm)
        cross_q = jnp.dot(normed, cross_wq, preferred_element_type=jnp.float32).astype(jnp.bfloat16)
        cross_q = rms_norm(cross_q.reshape(batch_rows, heads_local, head_dim), cross_qnorm)
        cross_mask = (xvalid > 0)[:, None, None, :]
        cross_stats = local_softmax(cross_q.reshape(batch_rows, kv_local, group_size, head_dim), k_cross, v_cross, cross_mask, score_scale)
        cross_attn = cross_stats[2] / cross_stats[1][..., None]
        cross_flat = cross_attn.astype(jnp.bfloat16).reshape(batch_rows, heads_local * head_dim)
        gate_vals = jnp.tanh(cross_gates.astype(jnp.float32))
        row_scale = rowmask.astype(jnp.float32)[:, None]
        xattn_sum = lax.psum(jnp.dot(cross_flat, cross_wo, preferred_element_type=jnp.float32), 'tp')
        after_cross = (after_mlp.astype(jnp.float32) + gate_vals[0] * row_scale * xattn_sum).astype(jnp.bfloat16)
        xmlp_sum = lax.psum(mlp_partial(rms_norm(after_cross, cross_mlp_norm), cross_wgate, cross_wup, cross_wdown), 'tp')
        after_xmlp = (after_cross.astype(jnp.float32) + gate_vals[1] * row_scale * xmlp_sum).astype(jnp.bfloat16)
        return after_xmlp, k_new_cache, v_new_cache

    return jax.shard_map(local_step, mesh=mesh, in_specs=in_specs, out_specs=out_specs, check_vma=False)
```

profile of v0, /device:TPU:0, one launch (start us, length us, event | category | flops | bytes accessed | tf_op | source)
XLA Modules:
  0.0 348.3 jit_solution(355434561683947511)
XLA Ops:
  9.4 1.6 fusion.37
  11.0 2.3 convolution_convert_fusion.6
  14.1 5.3 %fusion.36 = f32[8,8,8,128]{3,1,2,0:T(8,128)S(1)} fusion(bf16[4096,1024]{1,0:T(8,128)(2,1)} %param.35, bf16[64,4096]{1,0:T(8,128)(2,1)} %param.26, f32[4096]{0:T(1024)S(1)} %convert_element_type.158, f32[64]{0:T(128)S(1)} %add_rsqrt_fusion.4), kind=kOutput, calls=%fused_computation.48 | convolution fusion | flops 538050560 | bytes 9191680 | tf_op jit(solution)/shard_map/dot_general | solution.py:92
  20.2 6.7 %broadcast_select_fusion.1 = (bf16[64,64,2,128]{3,2,1,0:T(2,128)(2,1)S(1)}, bf16[64,64,2,128]{3,2,1,0:T(2,128)(2,1)}) fusion(bf16[64,64,2,128]{3,2,1,0:T(2,128)(2,1)S(1)} %copy-done.3, pred[64,64]{1,0:T(8,128)(4,1)S(1)} %get-tuple-element.24, bf16[64,2,128]{2,1,0:T(2,128)(2,1)S(1)} %pad_maximum_fusion, bf16[64,64,2,128]{3,2,1,0:T(2,128)(2,1)S(1)} %copy-done.4, ...), kind=kLoop, calls=%fused_computation.18 | loop fusion | flops 2097152 | bytes 8458240 | tf_op jit(solution)/shard_map/jit(_where)/select_n | solution.py:101
  28.3 21.6 %pmax.7 = f32[64,2,4]{2,1,0:T(2,128)S(1)} all-reduce(f32[64,2,4]{2,1,0:T(2,128)S(1)} %get-tuple-element.27), channel_id=1, replica_groups=mesh['dp'=2,'sp'=4,'tp'=4] {'sp'}, use_global_device_ids=true, to_apply=%region_2.3 | all-reduce | flops 512 | bytes 4096 | tf_op jit(solution)/shard_map/pmax | solution.py:60
  50.4 3.0 fusion.31
  53.5 16.9 %psum.43 = f32[64,2,4]{2,1,0:T(2,128)S(1)} all-reduce(f32[64,2,4]{2,1,0:T(2,128)S(1)} %bitcast.35), channel_id=1, replica_groups=mesh['dp'=2,'sp'=4,'tp'=4] {'sp'}, use_global_device_ids=true, to_apply=%region_5.6 | all-reduce | flops 512 | bytes 4096 | tf_op jit(solution)/shard_map/psum | solution.py:62
  70.3 17.2 %all-reduce.6.cloned.1.call-done = f32[64,2,4,128]{3,2,1,0:T(4,128)} async-done(((f32[64,2,4,128]{3,2,1,0:T(4,128)}), f32[64,2,4,128]{3,2,1,0:T(4,128)}) %all-reduce.6.cloned.1.call-update) | async-done | bytes 262160 | tf_op jit(solution)/shard_map/psum | solution.py:63
  88.8 6.0 %fusion.113 = f32[64,4096]{1,0:T(8,128)} fusion(bf16[64,1024]{1,0:T(8,128)(2,1)S(1)} %reshape.214, bf16[1024,4096]{1,0:T(8,128)(2,1)} %param.38), kind=kOutput, calls=%fused_computation.130 | convolution fusion | flops 536870912 | bytes 9568256 | tf_op jit(solution)/shard_map/dot_general | solution.py:107
  95.1 36.0 %all-reduce.8.cloned.1.call-done = f32[64,4096]{1,0:T(8,128)} async-done(((f32[64,4096]{1,0:T(8,128)}), f32[64,4096]{1,0:T(8,128)}) %all-reduce.8.cloned.1.call-update) | async-done | bytes 1048592 | tf_op jit(solution)/shard_map/psum | solution.py:107
  132.7 12.1 %fusion.12 = f32[64,3584]{1,0:T(8,128)S(1)} fusion(bf16[4096,3584]{1,0:T(8,128)(2,1)} %param.40, bf16[64,4096]{1,0:T(8,128)(2,1)S(1)} %get-tuple-element.8, f32[4096]{0:T(1024)S(1)} %convert_element_type.173, f32[64]{0:T(128)S(1)} %add_rsqrt_fusion.3), kind=kOutput, calls=%fused_computation.16 | convolution fusion | flops 1880555520 | bytes 30818560 | tf_op jit(solution)/shard_map/dot_general | solution.py:43
  144.8 23.1 %fusion.13 = f32[64,4096]{1,0:T(8,128)} fusion(bf16[3584,4096]{1,0:T(8,128)(2,1)} %param.42, bf16[4096,3584]{1,0:T(8,128)(2,1)} %param.41, f32[64,3584]{1,0:T(8,128)S(1)} %fusion.12, bf16[64,4096]{1,0:T(8,128)(2,1)S(1)} %get-tuple-element.8, f32[4096]{0:T(1024)S(1)} %convert_element_type.173, f32[64]{0:T(128)S(1)} %add_rsqrt_fusion.3), kind=kOutput, calls=%fused_computation.19 | convolution fusion | flops 3760979968 | bytes 61227264 | tf_op jit(solution)/shard_map/dot_general | solution.py:46
  168.0 36.7 %all-reduce.10.cloned.1.call-done = f32[64,4096]{1,0:T(8,128)} async-done(((f32[64,4096]{1,0:T(8,128)}), f32[64,4096]{1,0:T(8,128)}) %all-reduce.10.cloned.1.call-update) | async-done | bytes 1048592 | tf_op jit(solution)/shard_map/psum | solution.py:109
  206.2 5.0 %fusion.34 = f32[64,1024]{1,0:T(8,128)S(1)} fusion(bf16[4096,1024]{1,0:T(8,128)(2,1)} %param.44, bf16[64,4096]{1,0:T(8,128)(2,1)S(1)} %get-tuple-element.6, f32[4096]{0:T(1024)S(1)} %convert_element_type.183, f32[64]{0:T(128)S(1)} %add_rsqrt_fusion.2), kind=kOutput, calls=%fused_computation.45 | convolution fusion | flops 538050560 | bytes 9191680 | tf_op jit(solution)/shard_map/dot_general | solution.py:112
  211.8 5.9 %fusion.110 = (f32[64,2,4]{2,1,0:T(2,128)S(1)}, bf16[64,2,4,256]{3,2,1,0:T(4,128)(2,1)S(1)}) fusion(pred[64,256]{1,0:T(8,128)(4,1)S(1)} %broadcast_compare_fusion, bf16[64,256,2,128]{3,2,1,0:T(2,128)(2,1)} %param.30, f32[64,2,4,128]{3,2,1,0:T(4,128)S(1)} %reshape.218, f32[128]{0:T(128)S(1)} %convert_element_type.189, f32[64,2,4]{2,1,0:T(2,128)S(1)} %copy.47), kind=kOutput, calls=%fused_computation.129 | convolution fusion | flops 34537728 | bytes 8933888 | tf_op jit(solution)/shard_map/sub | solution.py:53
  217.7 4.6 %fusion.60 = bf16[64,2,4,128]{3,2,1,0:T(4,128)(2,1)S(1)} fusion(bf16[64,256,2,128]{3,2,1,0:T(2,128)(2,1)} %param.31, bf16[64,2,4,256]{3,2,1,0:T(4,128)(2,1)S(1)} %get-tuple-element.30, f32[64,2,4]{2,1,0:T(2,128)S(1)} %get-tuple-element.29), kind=kOutput, calls=%fused_computation.70 | convolution fusion | flops 33685504 | bytes 8783872 | tf_op jit(solution)/shard_map/bkgt,btkd->bkgd/dot_general | solution.py:55
  222.4 6.0 %fusion.114 = f32[64,4096]{1,0:T(8,128)} fusion(bf16[64,1024]{1,0:T(8,128)(2,1)S(1)} %reshape.215, bf16[1024,4096]{1,0:T(8,128)(2,1)} %param.46), kind=kOutput, calls=%fused_computation.131 | convolution fusion | flops 536870912 | bytes 9568256 | tf_op jit(solution)/shard_map/dot_general | solution.py:120
  229.3 1.8 convert_multiply_fusion.8
  231.1 34.1 %all-reduce.12.cloned.1.call-done = f32[64,4096]{1,0:T(8,128)} async-done(((f32[64,4096]{1,0:T(8,128)}), f32[64,4096]{1,0:T(8,128)}) %all-reduce.12.cloned.1.call-update) | async-done | bytes 1048592 | tf_op jit(solution)/shard_map/psum | solution.py:120
  265.2 1.6 fusion.53
  267.4 12.1 %fusion.8 = f32[64,3584]{1,0:T(8,128)S(1)} fusion(bf16[4096,3584]{1,0:T(8,128)(2,1)} %param.49, bf16[64,4096]{1,0:T(8,128)(2,1)S(1)} %get-tuple-element.4, f32[4096]{0:T(1024)S(1)} %convert_element_type.195, f32[64]{0:T(128)S(1)} %add_rsqrt_fusion.1), kind=kOutput, calls=%fused_computation.10 | convolution fusion | flops 1880555520 | bytes 30818560 | tf_op jit(solution)/shard_map/dot_general | solution.py:43
  279.5 23.2 %fusion.14 = f32[64,4096]{1,0:T(8,128)} fusion(bf16[3584,4096]{1,0:T(8,128)(2,1)} %param.51, bf16[4096,3584]{1,0:T(8,128)(2,1)} %param.50, f32[64,3584]{1,0:T(8,128)S(1)} %fusion.8, bf16[64,4096]{1,0:T(8,128)(2,1)S(1)} %get-tuple-element.4, f32[4096]{0:T(1024)S(1)} %convert_element_type.195, f32[64]{0:T(128)} %copy-done.7), kind=kOutput, calls=%fused_computation.20 | convolution fusion | flops 3760979968 | bytes 61227264 | tf_op jit(solution)/shard_map/dot_general | solution.py:46
  302.7 36.8 %all-reduce.14.cloned.1.call-done = f32[64,4096]{1,0:T(8,128)} async-done(((f32[64,4096]{1,0:T(8,128)}), f32[64,4096]{1,0:T(8,128)}) %all-reduce.14.cloned.1.call-update) | async-done | bytes 1048592 | tf_op jit(solution)/shard_map/psum | solution.py:122
  339.5 2.2 fusion.56
  (76 shorter events, 12.2 us)
Async XLA Ops:
  7.2 2.2 copy-start
  7.2 80.4 %all-reduce.6.cloned.1.call-start = ((), (), s32[]{:S(2)}) async-start(), calls=%async_computation | async-start | bytes 524288 | tf_op jit(solution)/shard_map/psum | solution.py:63
  14.1 6.1 %copy-start.3 = (bf16[64,64,2,128]{3,2,1,0:T(2,128)(2,1)S(1)}, bf16[64,64,2,128]{3,2,1,0:T(2,128)(2,1)}, u32[]{:S(2)}) copy-start(bf16[64,64,2,128]{3,2,1,0:T(2,128)(2,1)} %param.28) | copy-start | bytes 6291460
  14.1 6.1 %copy-start.4 = (bf16[64,64,2,128]{3,2,1,0:T(2,128)(2,1)S(1)}, bf16[64,64,2,128]{3,2,1,0:T(2,128)(2,1)}, u32[]{:S(2)}) copy-start(bf16[64,64,2,128]{3,2,1,0:T(2,128)(2,1)} %param.29) | copy-start | bytes 6291460
  26.9 61.8 %copy-start.5 = (bf16[64,64,2,128]{3,2,1,0:T(2,128)(2,1)}, bf16[64,64,2,128]{3,2,1,0:T(2,128)(2,1)S(1)}, u32[]{:S(2)}) copy-start(bf16[64,64,2,128]{3,2,1,0:T(2,128)(2,1)S(1)} %get-tuple-element.15) | copy-start | bytes 6291460
  53.4 77.7 %all-reduce.8.cloned.1.call-start = ((), (), s32[]{:S(2)}) async-start(), calls=%async_computation.1 | async-start | bytes 2097152 | tf_op jit(solution)/shard_map/psum | solution.py:107
  88.8 6.3 %copy-start.8 = (bf16[4096]{0:T(1024)(128)(2,1)S(1)}, bf16[4096]{0:T(1024)(128)(2,1)}, u32[]{:S(2)}) copy-start(bf16[4096]{0:T(1024)(128)(2,1)} %param.39) | copy-start | bytes 24580
  88.8 42.3 %copy-start.2 = (bf16[64,4096]{1,0:T(8,128)(2,1)S(1)}, bf16[64,4096]{1,0:T(8,128)(2,1)}, u32[]{:S(2)}) copy-start(bf16[64,4096]{1,0:T(8,128)(2,1)} %param.26) | copy-start | bytes 1572868
  94.9 109.8 %all-reduce.10.cloned.1.call-start = ((), (), s32[]{:S(2)}) async-start(), calls=%async_computation.2 | async-start | bytes 2097152 | tf_op jit(solution)/shard_map/psum | solution.py:109
  144.8 23.2 %copy-start.9 = (bf16[4096]{0:T(1024)(128)(2,1)S(1)}, bf16[4096]{0:T(1024)(128)(2,1)}, u32[]{:S(2)}) copy-start(bf16[4096]{0:T(1024)(128)(2,1)} %param.43) | copy-start | bytes 24580
  144.8 23.2 %copy-start.12 = (bf16[128]{0:T(256)(128)(2,1)S(1)}, bf16[128]{0:T(256)(128)(2,1)}, u32[]{:S(2)}) copy-start(bf16[128]{0:T(256)(128)(2,1)} %param.45) | copy-start | bytes 772
  144.8 23.2 %copy-start.6 = (s32[64,256]{1,0:T(8,128)S(1)}, s32[64,256]{1,0:T(8,128)}, u32[]{:S(2)}) copy-start(s32[64,256]{1,0:T(8,128)} %param.32) | copy-start | bytes 196612
  167.9 97.3 %all-reduce.12.cloned.1.call-start = ((), (), s32[]{:S(2)}) async-start(), calls=%async_computation.3 | async-start | bytes 2097152 | tf_op jit(solution)/shard_map/psum | solution.py:120
  222.4 6.3 %copy-start.13 = (f32[2]{0:T(128)S(1)}, f32[2]{0:T(128)}, u32[]{:S(2)}) copy-start(f32[2]{0:T(128)} %param.47) | copy-start | bytes 28
  222.4 6.3 %copy-start.10 = (bf16[4096]{0:T(1024)(128)(2,1)S(1)}, bf16[4096]{0:T(1024)(128)(2,1)}, u32[]{:S(2)}) copy-start(bf16[4096]{0:T(1024)(128)(2,1)} %param.48) | copy-start | bytes 24580
  222.4 6.9 %copy-start.11 = (s32[64]{0:T(128)S(1)}, s32[64]{0:T(128)}, u32[]{:S(2)}) copy-start(s32[64]{0:T(128)} %param.33) | copy-start | bytes 772
  228.4 111.1 %all-reduce.14.cloned.1.call-start = ((), (), s32[]{:S(2)}) async-start(), calls=%async_computation.4 | async-start | bytes 2097152 | tf_op jit(solution)/shard_map/psum | solution.py:122
  266.8 0.5 copy-start.7
  279.5 62.3 %copy-start.1 = (bf16[4096,256]{1,0:T(8,128)(2,1)S(1)}, bf16[4096,256]{1,0:T(8,128)(2,1)}, u32[]{:S(2)}) copy-start(bf16[4096,256]{1,0:T(8,128)(2,1)} %param.36) | copy-start | bytes 6291460
Sparse Core Ops, SparseCore 0:
  53.5 33.9 all-reduce.5
  95.0 36.0 all-reduce.7
  168.0 36.6 all-reduce.9
  228.6 36.6 all-reduce.11
  302.9 36.6 all-reduce.13
where the time goes:
time: 349 us; the launch traced here: 348 us
  waiting for transfers between devices  161 us (46%)
  matrix products  112 us (32%)
  blocking collectives  38.4 us (11%)
  other arithmetic  20.6 us (6%)
  between operations  14.3 us (4%)
    dot_general x2, matrix products, mlp_partial(): return jnp.dot(hidden_act, w_down, preferred_element_type=jnp.float32)  46.3 us
    psum x1, waiting for transfers between devices, local_step(): lax.psum(mlp_partial(rms_norm(after_cross, cross_mlp_norm), cross_wgate,...  36.8 us
    psum x1, waiting for transfers between devices, local_step(): lax.psum(mlp_partial(rms_norm(after_attn, self_mlp_norm), self_wgate, sel...  36.7 us
    psum x1, waiting for transfers between devices, local_step(): lax.psum(jnp.dot(self_flat, self_wo, preferred_element_type=jnp.float32),...  36 us
    psum x1, waiting for transfers between devices, local_step(): lax.psum(jnp.dot(cross_flat, cross_wo, preferred_element_type=jnp.float32...  34.1 us
    dot_general x2, matrix products, mlp_partial(): jnp.dot(normed, w_gate, preferred_element_type=jnp.float32)  24.2 us
    pmax x1, blocking collectives, combine_sp(): glob_max = lax.pmax(part_max, 'sp')  21.6 us
    psum x1, waiting for transfers between devices, combine_sp(): total_out = lax.psum(part_out * factor[..., None], 'sp')  17.2 us
  transfers between devices with their start and end apart: 5, of which 5 were waited for; matrix products, arithmetic and copies ran while one was open for 1% of the time, Pallas kernels for 0%

commit v1 on v0

v1 whole, which is shorter than its diff:
```python
import math
import numpy as np
import jax
import jax.numpy as jnp
from jax import lax
from jax.experimental import pallas as pl
from jax.experimental.pallas import tpu as pltpu
from jax.sharding import PartitionSpec as P

NORM_EPS = 1e-5
ROPE_THETA = 500000.0
ROPE_FACTOR = 8.0
LOW_FREQ = 1.0
HIGH_FREQ = 4.0
ORIG_CTX = 8192.0
NEG_BIG = -1e30
F32 = jnp.float32
BF16 = jnp.bfloat16
MESH_ID = pl.DeviceIdType.MESH

CW = 256
HD = 128
NH = 8
NQ = 4
ROWS = 64
NSP = 4
RB = 16
TBLK = 64
WIDTH = 4096
UNROLL = 8
VMEM_ALL = 67043328
NCH = 16
FF = 3584
QW = 1024
BLK3 = (RB, NH, HD)
NPAIR = 11
SEG_WO = (0, 2)
SEG_GU = (2, 14)
SEG_DN = (16, 8)
SEG_CQ = (24, 2)
SEG_CWO = (26, 2)
SEG_CGU = (28, 14)
SEG_CDN = (42, 8)


def rope_freqs(head_dim):
    f32 = np.float32
    inv_freq = (1.0 / (f32(ROPE_THETA) ** (np.arange(0, head_dim, 2).astype(f32) / f32(head_dim)))).astype(f32)
    wavelen = 2.0 * math.pi / inv_freq
    smooth = (ORIG_CTX / wavelen - LOW_FREQ) / (HIGH_FREQ - LOW_FREQ)
    mid_freq = (1.0 - smooth) * inv_freq / ROPE_FACTOR + smooth * inv_freq
    scaled = np.where(wavelen > ORIG_CTX / LOW_FREQ, inv_freq / ROPE_FACTOR, mid_freq)
    return np.where(wavelen < ORIG_CTX / HIGH_FREQ, inv_freq, scaled).astype(f32)


def blk(i, n):
    return pl.ds(pl.multiple_of(i * n, n), n)


def half_of(n, core):
    return pl.ds(n * 4 + 2 * core, 2)


def round_bf16(x):
    return x.astype(BF16).astype(F32)


def attend(queries, keys, values, limits, scale):
    scores = [lax.dot_general(q, k, (((1,), (1,)), ((), ())), preferred_element_type=F32)
              for q, k in zip(queries, keys)]
    lane = lax.broadcasted_iota(jnp.int32, scores[0].shape, 1)
    head = lax.broadcasted_iota(jnp.int32, scores[0].shape, 0)
    own = (lane & 1) == (head >> 2)
    slot = lane >> 1
    oks = [own & (slot < limit) for limit in limits]
    scores = [jnp.where(ok, sc * scale, NEG_BIG) for ok, sc in zip(oks, scores)]
    maxes = [jnp.max(sc, axis=1, keepdims=True) for sc in scores]
    probs = [jnp.where(ok, jnp.exp(sc - m), 0.0) for ok, sc, m in zip(oks, scores, maxes)]
    sums = [jnp.sum(p, axis=1, keepdims=True) for p in probs]
    outs = [jnp.dot(p.astype(BF16), v, preferred_element_type=F32) for p, v in zip(probs, values)]
    return maxes, sums, outs


def front_kernel(pos_ref, hid_hbm, g_ref, freq_ref, wq, wk, wv, k_hbm, v_hbm,
                 k_out, v_out, o_ref, st_ref,
                 hid, x, wbuf, kbuf, vbuf, qkv, gsc, tab, cosb, sinb,
                 wsem, hsem, ksem, vsem, kosem, vosem):
    base = lax.axis_index('sp') * TBLK
    hc = pltpu.make_async_copy(hid_hbm, hid, hsem)
    hc.start()
    for i in range(NQ):
        pltpu.make_async_copy(wq.at[:, pl.ds(i * CW, CW)], wbuf.at[i], wsem.at[i]).start(priority=1)
    pltpu.make_async_copy(wk, wbuf.at[NQ], wsem.at[NQ]).start(priority=1)
    pltpu.make_async_copy(wv, wbuf.at[NQ + 1], wsem.at[NQ + 1]).start(priority=1)

    def cache_copies(j, out):
        rows = pl.ds(j * RB, RB)
        if out:
            return (pltpu.make_async_copy(kbuf.at[rows], k_out.at[rows], kosem.at[j]),
                    pltpu.make_async_copy(vbuf.at[rows], v_out.at[rows], vosem.at[j]))
        return (pltpu.make_async_copy(k_hbm.at[rows], kbuf.at[rows], ksem.at[j]),
                pltpu.make_async_copy(v_hbm.at[rows], vbuf.at[rows], vsem.at[j]))

    for j in range(NSP):
        for cp in cache_copies(j, False):
            cp.start(priority=1)
    with jax.named_scope('tables'):
        gsc[...] = g_ref[...].astype(F32)

        def fill(r, carry):
            tab[pl.ds(r, 1), :] = jnp.full((1, HD), pos_ref[r], jnp.int32).astype(F32)
            return carry

        lax.fori_loop(0, ROWS, fill, 0, unroll=8)
        angle = tab[...] * freq_ref[...]
        lanes = lax.broadcasted_iota(jnp.int32, (ROWS, HD), 1)
        sin_v = jnp.sin(angle)
        cosb[...] = jnp.cos(angle)
        sinb[...] = jnp.where(lanes < HD // 2, -sin_v, sin_v)

    with jax.named_scope('norm'):
        hc.wait()

        def norm_rows(r, carry):
            rows = blk(r, RB)
            acc = jnp.zeros((RB, HD), F32)
            for j in range(WIDTH // HD):
                v = hid[rows, j * HD:(j + 1) * HD].astype(F32)
                acc = acc + v * v
            inv = lax.rsqrt(jnp.sum(acc, axis=-1, keepdims=True) * (1.0 / WIDTH) + NORM_EPS)
            for j in range(WIDTH // HD):
                cs = slice(j * HD, (j + 1) * HD)
                x[rows, cs] = (hid[rows, cs].astype(F32) * inv * gsc[j:j + 1, :]).astype(BF16)
            return carry

        lax.fori_loop(0, NSP, norm_rows, 0)

    with jax.named_scope('qkv'):
        def project(p, carry):
            for v in range(2):
                pltpu.make_async_copy(wk, wbuf.at[2 * p + v], wsem.at[2 * p + v]).wait()
            ys = [jnp.dot(x[...], wbuf[2 * p + v], preferred_element_type=F32) for v in range(2)]
            for v in range(2):
                yv = round_bf16(ys[v])
                for u in range(2):
                    part = yv[:, u * HD:(u + 1) * HD]
                    turned = round_bf16(part * cosb[...] + pltpu.roll(part, HD // 2, 1) * sinb[...])
                    if v == 1:
                        turned = jnp.where(p == NQ // 2, part, turned)
                    qkv[pl.ds(4 * p + 2 * v + u, ROWS, stride=RB), :] = turned
            return carry

        lax.fori_loop(0, NQ // 2 + 1, project, 0)

    scale = HD ** -0.5
    row_t = lax.broadcasted_iota(jnp.int32, (HD, HD), 0)
    lane8 = lax.broadcasted_iota(jnp.int32, (NH, HD), 1)
    head8 = lax.broadcasted_iota(jnp.int32, (NH, HD), 0)

    def put(buf, pair, b, lp):
        both = jnp.where((row_t & 1) == 0, pair[0:1, :], pair[1:2, :])
        upd = jnp.where((row_t >> 1) == lp, both, buf[b].astype(F32)).astype(BF16)
        buf[b] = upd
        return upd

    def some_rows(rows):
        lps = [pos_ref[b] - base for b in rows]
        fresh = [qkv[pl.ds(pl.multiple_of(b * RB + NH, NH), NH), :] for b in rows]
        queries = [qkv[pl.ds(pl.multiple_of(b * RB, RB), NH), :].astype(BF16) for b in rows]
        keys = [put(kbuf, f[0:2], b, lp) for f, b, lp in zip(fresh, rows, lps)]
        values = [put(vbuf, f[2:4], b, lp) for f, b, lp in zip(fresh, rows, lps)]
        maxes, sums, outs = attend(queries, keys, values, [lp + 1 for lp in lps], scale)
        for b, m, l, o in zip(rows, maxes, sums, outs):
            o_ref[blk(b, NH), :] = o
            st = jnp.where(lane8 == head8, m, 0.0) + jnp.where(lane8 == head8 + NH, l, 0.0)
            st_ref[pl.ds(b, 1), :] = jnp.sum(st, axis=0, keepdims=True)

    with jax.named_scope('attend'):
        def block(j, carry):
            for cp in cache_copies(j, False):
                cp.wait()

            def some(i, carry2):
                some_rows([j * RB + i * UNROLL + u for u in range(UNROLL)])
                return carry2

            lax.fori_loop(0, RB // UNROLL, some, 0)
            for cp in cache_copies(j, True):
                cp.start()
            return carry

        lax.fori_loop(0, NSP, block, 0)
    with jax.named_scope('flush'):
        for j in range(NSP):
            for cp in cache_copies(j, True):
                cp.wait()


def back_kernel(mask_ref, gates_ref, o_part, stats, hid_hbm, xv_hbm, g2_ref, g3_ref, g4_ref, qn_ref,
                wo, wg, wu, wd, cq, cwo, cg, cu, cd, kc_hbm, vc_hbm,
                out_ref,
                ring, kc, vc, hidb, xvb, cnt, gab, gmb, gsc, hres, xb, ab, ofl, osc, qsc, ro, rst, pb, r1, sb, r2, tb, full,
                rsem, csem, hsem, xsem, osem, stsem, a1s, a1r, a2s, a2r, a3s, a3r, zss, zrs, yss, yrs, dss, drs):
    s = lax.axis_index('sp')
    t = lax.axis_index('tp')
    c = lax.rem(t, 2)
    y = lax.div(t, 2)
    core_peer = {'tp': t + 1 - 2 * c}
    y_peer = {'tp': lax.rem(t + 2, 4)}
    sp_peers = [lax.rem(s + k, 4) for k in (1, 2, 3)]
    sp_from = [lax.rem(s + 4 - k, 4) for k in (1, 2, 3)]

    def cols(w, j):
        return w.at[:, blk(j, CW)]

    def tall(w, slot, sub, j):
        return [(cols(w, j), ring.at[slot, sub, pl.ds(0, w.shape[0])])]

    def square(w, slot, sub, j):
        rows = w.shape[0]
        return [(cols(w, 4 * j + k), ring.at[slot, sub, pl.ds(k * rows, rows)]) for k in range(4)]

    segments = (
        (SEG_WO, lambda sl, p: square(wo, sl, 0, 2 * p), lambda sl, p: square(wo, sl, 1, 2 * p + 1)),
        (SEG_GU, lambda sl, p: tall(wg, sl, 0, p), lambda sl, p: tall(wu, sl, 1, p)),
        (SEG_DN, lambda sl, p: tall(wd, sl, 0, 2 * p), lambda sl, p: tall(wd, sl, 1, 2 * p + 1)),
        (SEG_CQ, lambda sl, p: tall(cq, sl, 0, 2 * p), lambda sl, p: tall(cq, sl, 1, 2 * p + 1)),
        (SEG_CWO, lambda sl, p: square(cwo, sl, 0, 2 * p), lambda sl, p: square(cwo, sl, 1, 2 * p + 1)),
        (SEG_CGU, lambda sl, p: tall(cg, sl, 0, p), lambda sl, p: tall(cu, sl, 1, p)),
        (SEG_CDN, lambda sl, p: tall(cd, sl, 0, 2 * p), lambda sl, p: tall(cd, sl, 1, 2 * p + 1)),
    )

    def issue(pair, low, high):
        slot = lax.rem(pair, NPAIR)
        for (first, count), even, odd in segments:
            if first >= high or first + count <= low:
                continue

            def go(first=first, even=even, odd=odd):
                for sub, make in ((0, even), (1, odd)):
                    for src, dst in make(slot, pair - first):
                        pltpu.make_async_copy(src, dst, rsem.at[slot, sub]).start(priority=1)

            if first <= low and high <= first + count:
                go()
            else:
                pl.when((pair >= first) & (pair < first + count))(go)

    def arrive(slot, sub, rows):
        dst = ring.at[slot, sub, pl.ds(0, rows)]
        pltpu.make_async_copy(dst, dst, rsem.at[slot, sub]).wait()

    def send1(ar, n):
        return pltpu.make_async_remote_copy(
            pb.at[ar, half_of(n, 1 - c)], r1.at[ar, n], a1s.at[ar, n], a1r.at[ar, n],
            device_id=core_peer, device_id_type=MESH_ID)

    def send2(ar, n):
        return pltpu.make_async_remote_copy(
            sb.at[ar, n], r2.at[ar, n], a2s.at[ar, n], a2r.at[ar, n],
            device_id=y_peer, device_id_type=MESH_ID)

    def send3(ar, n):
        mine = tb.at[ar, half_of(n, c)]
        return pltpu.make_async_remote_copy(
            mine, mine, a3s.at[ar, n], a3r.at[ar, n], device_id=core_peer, device_id_type=MESH_ID)

    def stage2(ar, n):
        send1(ar, n).wait_recv()
        sb[ar, n] = pb[ar, half_of(n, c)] + r1[ar, n]
        send2(ar, n).start()

    def stage3(ar, n):
        send2(ar, n).wait_recv()
        tb[ar, half_of(n, c)] = sb[ar, n] + r2[ar, n]
        send3(ar, n).start()

    def to_sp(n, k):
        mine = full.at[s, half_of(n, c)]
        i = lax.div(n, 2)
        return pltpu.make_async_remote_copy(
            mine, mine, zss.at[i, k], zrs.at[i, k], device_id={'sp': sp_peers[k]}, device_id_type=MESH_ID)

    def from_sp(i, k):
        got = full.at[sp_from[k], half_of(2 * i + y, c)]
        return got, pltpu.make_async_remote_copy(
            got, got, zss.at[i, k], zrs.at[i, k], device_id={'sp': sp_peers[k]}, device_id_type=MESH_ID)

    def to_y(i, k):
        got = full.at[sp_from[k], half_of(2 * i + y, c)]
        return pltpu.make_async_remote_copy(
            got, got, yss.at[i, k], yrs.at[i, k], device_id=y_peer, device_id_type=MESH_ID)

    def to_core(piece, idx):
        return pltpu.make_async_remote_copy(
            piece, piece, dss.at[idx], drs.at[idx], device_id=core_peer, device_id_type=MESH_ID)

    def own_piece(n):
        return full.at[s, half_of(n, c)]

    def final3(ar, n):
        send2(ar, n).wait_recv()
        gm = gmb[...]
        for u in range(2):
            piece = n * 4 + 2 * c + u
            total = sb[ar, n, u] + r2[ar, n, u]
            for w in range(2):
                cs = slice(w * HD, (w + 1) * HD)
                full[s, piece, :, cs] = round_bf16(hres[piece][:, cs] + gm * total[:, cs])
        to_core(own_piece(n), n).start()

        @pl.when(lax.rem(n, 2) == y)
        def _():
            for k in range(3):
                to_sp(n, k).start()

    def advance(ar, n, last=False):
        send1(ar, n).start()

        @pl.when(n >= 1)
        def _():
            stage2(ar, n - 1)

        @pl.when(n >= 2)
        def _():
            (final3 if last else stage3)(ar, n - 2)

    def drain(ar, last=False):
        third = final3 if last else stage3
        third(ar, 2)
        third(ar, 3)
        for n in range(4):
            if not last:
                send3(ar, n).wait_recv()
            send1(ar, n).wait_send()
            send2(ar, n).wait_send()
            if not last:
                send3(ar, n).wait_send()

    def norm(g_ref, update):
        gsc[...] = g_ref[...].astype(F32)

        def add(q, acc):
            v = update(q)
            hres[q] = v
            return acc + v * v

        acc = lax.fori_loop(0, NCH, add, jnp.zeros((RB, CW), F32), unroll=4)
        inv = lax.rsqrt(jnp.sum(acc, axis=-1, keepdims=True) * (1.0 / WIDTH) + NORM_EPS)

        def put(q, carry):
            for u in range(2):
                cs = slice(u * HD, (u + 1) * HD)
                v = hres[q][:, cs] * inv * gsc[pl.ds(2 * q + u, 1), :]
                xb[:, pl.ds(pl.multiple_of(q * CW + u * HD, HD), HD)] = v.astype(BF16)
            return carry

        lax.fori_loop(0, NCH, put, 0, unroll=4)

    def project_out(ar, seg):
        first = seg[0]

        def pair(p, carry):
            slot = lax.rem(first + p, NPAIR)
            for sub in range(2):
                n = 2 * p + sub
                arrive(slot, sub, WIDTH)
                ps = [jnp.dot(ofl[...], ring[slot, sub, k * QW:(k + 1) * QW, :], preferred_element_type=F32)
                      for k in range(4)]
                for k in range(4):
                    pb[ar, n * 4 + k] = ps[k]
                send1(ar, n).start()
            issue(first + p + NPAIR, first + NPAIR, first + NPAIR + 2)
            return carry

        lax.fori_loop(0, 2, pair, 0)
        for n in range(3):
            stage2(ar, n)
        stage2(ar, 3)
        stage3(ar, 0)
        stage3(ar, 1)
        drain(ar)

    def gate_up(seg):
        first = seg[0]

        def pair(p, carry):
            slot = lax.rem(first + p, NPAIR)
            for sub in range(2):
                arrive(slot, sub, WIDTH)
            gate, up = [jnp.dot(xb[...], ring[slot, sub], preferred_element_type=F32) for sub in range(2)]
            gate, up = round_bf16(gate), round_bf16(up)
            act = (gate * jax.nn.sigmoid(gate) * up).astype(BF16)
            ab[:, blk(p, CW)] = act
            issue(first + p + NPAIR, first + NPAIR, first + NPAIR + seg[1])
            return carry

        lax.fori_loop(0, seg[1], pair, 0)

    def down(ar, seg, last=False):
        first = seg[0]

        def group(n, carry):
            def pair(p, carry2):
                idx = first + 2 * n + p
                slot = lax.rem(idx, NPAIR)
                for sub in range(2):
                    arrive(slot, sub, FF)
                both = [jnp.dot(ab[...], ring[slot, sub, :FF, :], preferred_element_type=F32) for sub in range(2)]
                for sub in range(2):
                    pb[ar, n * 4 + 2 * p + sub] = both[sub]
                if not last:
                    issue(idx + NPAIR, first + NPAIR, first + NPAIR + seg[1])
                return carry2

            lax.fori_loop(0, 2, pair, 0)
            advance(ar, n, last)
            return carry

        lax.fori_loop(0, 4, group, 0)
        stage2(ar, 3)
        drain(ar, last)

    def heads_to_rows():
        for h in range(8):
            ofl[:, h * 128:(h + 1) * 128] = osc[pl.ds(h, 16, stride=8), :].astype(BF16)

    hcopy = pltpu.make_async_copy(hid_hbm.at[blk(s, RB)], hidb, hsem)
    hcopy.start()
    xcopy = pltpu.make_async_copy(xv_hbm.at[blk(s, RB)], xvb, xsem)
    xcopy.start()
    for p in range(5):
        issue(p, p, p + 1)
    barrier = pltpu.get_barrier_semaphore()
    for peer in [core_peer, y_peer] + [{'sp': v} for v in sp_peers]:
        pl.semaphore_signal(barrier, inc=1, device_id=peer, device_id_type=MESH_ID)
    pl.semaphore_wait(barrier, 5)

    def part_copy(k):
        rows = blk(sp_peers[k], HD)
        srow = blk(sp_peers[k], RB)
        to = {'sp': sp_peers[k]}
        return (pltpu.make_async_remote_copy(o_part.at[rows], ro.at[k], osem.at[0, k], osem.at[1, k],
                                             device_id=to, device_id_type=MESH_ID),
                pltpu.make_async_remote_copy(stats.at[srow], rst.at[k], stsem.at[0, k], stsem.at[1, k],
                                             device_id=to, device_id_type=MESH_ID))

    for k in (2, 1, 0):
        for cp in part_copy(k):
            cp.start()
    for p in range(5, NPAIR):
        issue(p, p, p + 1)
    for r in range(RB):
        on = jnp.full((1, HD), mask_ref[s * RB + r], jnp.int32).astype(F32)
        gab[r:r + 1, :] = on
    on = gab[...]
    gab[...] = jnp.tanh(jnp.full((RB, HD), gates_ref[0], F32)) * on
    gmb[...] = jnp.tanh(jnp.full((RB, HD), gates_ref[1], F32)) * on
    xcopy.wait()
    cnt[...] = jnp.broadcast_to(jnp.sum((xvb[...] > 0).astype(jnp.int32), axis=1, keepdims=True), (RB, HD))
    with jax.named_scope('parts'):
        for k in range(3):
            for cp in part_copy(k):
                cp.wait()

    lane3 = lax.broadcasted_iota(jnp.int32, BLK3, 2)
    head3 = lax.broadcasted_iota(jnp.int32, BLK3, 1)

    def pick(st, off):
        return jnp.sum(jnp.where(lane3 == head3 + off, st[:, None, :], 0.0), axis=2, keepdims=True)

    parts = [(o_part[blk(s, HD), :], stats[blk(s, RB), :])]
    parts += [(ro[k], rst[k]) for k in range(3)]
    maxes = [pick(st, 0) for _, st in parts]
    top = jnp.maximum(jnp.maximum(maxes[0], maxes[1]), jnp.maximum(maxes[2], maxes[3]))
    total = jnp.zeros(BLK3, F32)
    denom = jnp.zeros((16, 8, 1), F32)
    for (o, st), m in zip(parts, maxes):
        f = jnp.exp(m - top)
        denom = denom + pick(st, 8) * f
        total = total + o.reshape(BLK3) * f
    osc[...] = (total / denom).reshape(HD, HD)
    heads_to_rows()
    hcopy.wait()

    with jax.named_scope('wo'):
        project_out(0, SEG_WO)
    with jax.named_scope('norm2'):
        norm(g2_ref, lambda q: round_bf16(
            hidb[:, blk(q, CW)].astype(F32) + tb[0, q]))
    with jax.named_scope('gu'):
        gate_up(SEG_GU)
    rows16 = blk(s, RB)
    kcopy = pltpu.make_async_copy(kc_hbm.at[rows16], kc, csem.at[0])
    vcopy = pltpu.make_async_copy(vc_hbm.at[rows16], vc, csem.at[1])
    kcopy.start(priority=1)
    vcopy.start(priority=1)
    with jax.named_scope('dn'):
        down(1, SEG_DN)
    with jax.named_scope('norm3'):
        norm(g3_ref, lambda q: round_bf16(hres[q] + tb[1, q]))

    qn = qn_ref[...].astype(F32)
    first_q = SEG_CQ[0]
    with jax.named_scope('cq'):
        def queries(p, carry):
            slot = lax.rem(first_q + p, NPAIR)
            for sub in range(2):
                arrive(slot, sub, WIDTH)
            both = [jnp.dot(xb[...], ring[slot, sub], preferred_element_type=F32) for sub in range(2)]
            for sub in range(2):
                part = round_bf16(both[sub])
                for u in range(2):
                    v = part[:, u * HD:(u + 1) * HD]
                    inv = lax.rsqrt(jnp.mean(v * v, axis=-1, keepdims=True) + NORM_EPS)
                    qsc[pl.ds(4 * p + 2 * sub + u, RB, stride=NH), :] = round_bf16(v * inv * qn)
            issue(first_q + p + NPAIR, first_q + NPAIR, first_q + NPAIR + 2)
            return carry

        lax.fori_loop(0, 2, queries, 0)

    with jax.named_scope('cross'):
        kcopy.wait()
        vcopy.wait()

        def cross_rows(i, carry):
            bs = [i * 4 + u for u in range(4)]
            rows = [blk(b, NH) for b in bs]
            _, sums, outs = attend([qsc[r, :].astype(BF16) for r in rows], [kc[b] for b in bs], [vc[b] for b in bs],
                                   [cnt[pl.ds(b, 1), 0:1] for b in bs], HD ** -0.5)
            for r, l, o in zip(rows, sums, outs):
                osc[r, :] = o / l
            return carry

        lax.fori_loop(0, 4, cross_rows, 0)
        heads_to_rows()
    with jax.named_scope('cwo'):
        project_out(2, SEG_CWO)
    with jax.named_scope('norm4'):
        ga = jnp.concatenate([gab[...], gab[...]], axis=1)
        norm(g4_ref, lambda q: round_bf16(hres[q] + ga * tb[2, q]))
    with jax.named_scope('cgu'):
        gate_up(SEG_CGU)
    with jax.named_scope('cdn'):
        down(3, SEG_CDN, last=True)

    with jax.named_scope('spread'):
        for i in range(2):
            for k in range(3):
                got, cp = from_sp(i, k)
                cp.wait_recv()
                to_y(i, k).start()
                to_core(got, 4 + 3 * i + k).start()
        for i in range(2):
            for k in range(3):
                to_y(i, k).wait_recv()
                other = full.at[sp_from[k], half_of(2 * i + 1 - y, c)]
                to_core(other, 10 + 3 * i + k).start()
        for idx in range(16):
            to_core(own_piece(0), idx).wait()
        for i in range(2):
            for k in range(3):
                to_sp(2 * i, k).wait_send()
                to_y(i, k).wait_send()
    with jax.named_scope('emit'):
        def emit(q, carry):
            for r in range(NSP):
                out_ref[r * RB:(r + 1) * RB, blk(q, CW)] = full[r, q].astype(BF16)
            return carry

        lax.fori_loop(0, NCH, emit, 0, unroll=2)


def solution(mesh):
    cache_spec = P('dp', 'sp', 'tp', None)
    cross_spec = P('dp', None, 'tp', None)
    row_spec = P('dp', None)
    vec_spec = P('dp')
    full_spec = P(None)
    col_spec = P(None, 'tp')
    split_rows = P('tp', None)
    in_specs = (row_spec, vec_spec, cache_spec, cache_spec, cross_spec, cross_spec, row_spec, vec_spec,
                full_spec, col_spec, col_spec, col_spec, split_rows, full_spec, col_spec, col_spec, split_rows,
                full_spec, col_spec, full_spec, split_rows, full_spec, full_spec, col_spec, col_spec, split_rows)
    out_specs = (row_spec, cache_spec, cache_spec)
    vmem = pl.BlockSpec(memory_space=pltpu.VMEM)
    smem = pl.BlockSpec(memory_space=pltpu.SMEM)
    hbm = pl.BlockSpec(memory_space=pl.ANY)
    dma = pltpu.SemaphoreType.DMA

    def local_step(hidden, new_pos, k_self, v_self, k_cross, v_cross, xvalid, rowmask,
                   self_attn_norm, self_wq, self_wk, self_wv, self_wo, self_mlp_norm,
                   self_wgate, self_wup, self_wdown, cross_attn_norm, cross_wq, cross_qnorm,
                   cross_wo, cross_gates, cross_mlp_norm, cross_wgate, cross_wup, cross_wdown):
        half = rope_freqs(HD)
        freq = np.concatenate([half, half]).reshape(1, HD).astype(np.float32)

        def fold(gain):
            return gain.reshape(WIDTH // HD, HD)

        k_new, v_new, o_part, stats = pl.pallas_call(
            front_kernel,
            out_shape=(*[jax.ShapeDtypeStruct((ROWS, HD, HD), BF16)] * 2,
                       jax.ShapeDtypeStruct((ROWS * NH, HD), F32), jax.ShapeDtypeStruct((ROWS, HD), F32)),
            in_specs=[smem, hbm, vmem, vmem, hbm, hbm, hbm, hbm, hbm],
            out_specs=(hbm, hbm, vmem, vmem),
            scratch_shapes=[
                *[pltpu.VMEM((ROWS, WIDTH), BF16)] * 2, pltpu.VMEM((NQ + 2, WIDTH, CW), BF16),
                *[pltpu.VMEM((ROWS, HD, HD), BF16)] * 2,
                pltpu.VMEM((ROWS * RB, HD), F32), pltpu.VMEM((WIDTH // HD, HD), F32),
                *[pltpu.VMEM((ROWS, HD), F32)] * 3,
                dma((NQ + 2,)), dma, *[dma((NSP,))] * 4],
            compiler_params=pltpu.CompilerParams(vmem_limit_bytes=VMEM_ALL),
            name='front',
        )(new_pos, hidden, fold(self_attn_norm), jnp.asarray(freq), self_wq, self_wk, self_wv,
          k_self.reshape(ROWS, HD, HD), v_self.reshape(ROWS, HD, HD))

        out = pl.pallas_call(
            back_kernel,
            out_shape=jax.ShapeDtypeStruct((ROWS, WIDTH), BF16),
            in_specs=[smem, smem, vmem, vmem, hbm, hbm] + [vmem] * 4 + [hbm] * 11,
            out_specs=vmem,
            scratch_shapes=[
                pltpu.VMEM((NPAIR, 2, WIDTH, CW), BF16),
                *[pltpu.VMEM((RB, 512, HD), BF16)] * 2,
                pltpu.VMEM((RB, WIDTH), BF16), pltpu.VMEM((RB, 256), jnp.int32), pltpu.VMEM((RB, HD), jnp.int32),
                pltpu.VMEM((RB, HD), F32), pltpu.VMEM((RB, HD), F32), pltpu.VMEM((WIDTH // HD, HD), F32),
                pltpu.VMEM((NCH, RB, CW), F32),
                pltpu.VMEM((RB, WIDTH), BF16), pltpu.VMEM((RB, FF), BF16), pltpu.VMEM((RB, QW), BF16),
                *[pltpu.VMEM((HD, HD), F32)] * 2, pltpu.VMEM((3, HD, HD), F32), pltpu.VMEM((3, RB, HD), F32),
                pltpu.VMEM((4, NCH, RB, CW), F32), *[pltpu.VMEM((4, 4, 2, RB, CW), F32)] * 3,
                *[pltpu.VMEM((4, NCH, RB, CW), F32)] * 2,
                dma((NPAIR, 2)), dma((2,)), dma, dma, *[dma((2, 3))] * 2,
                *[dma((4, 4))] * 6,
                *[dma((2, 3))] * 4, dma((NCH,)), dma((NCH,))],
            compiler_params=pltpu.CompilerParams(
                collective_id=0, has_side_effects=True, vmem_limit_bytes=VMEM_ALL),
            name='back',
        )(rowmask, cross_gates, o_part, stats, hidden, xvalid, fold(self_mlp_norm), fold(cross_attn_norm),
          fold(cross_mlp_norm), cross_qnorm.reshape(1, -1),
          self_wo, self_wgate, self_wup, self_wdown, cross_wq, cross_wo, cross_wgate, cross_wup, cross_wdown,
          *[cache.reshape(ROWS, -1, HD) for cache in (k_cross, v_cross)])
        return out, k_new.reshape(k_self.shape), v_new.reshape(v_self.shape)

    return jax.shard_map(local_step, mesh=mesh, in_specs=in_specs, out_specs=out_specs, check_vma=False)
```

time: 349 us -> 100 us (0.29)
  waiting for transfers between devices: 161 us -> 0 us
  matrix products: 112 us -> 0 us
  Pallas kernels: 0 us -> 97.6 us
  blocking collectives: 38.4 us -> 0 us
  other arithmetic: 20.6 us -> 0 us
  between operations: 14.3 us -> 0.65 us
    psum x5 -> x0, waiting for transfers between devices: 161 us -> none  [the longest x1 36.8 us: local_step(): lax.psum(mlp_partial(rms_norm(after_cross, cross_mlp_norm), cross_wgate,...]
    dot_general x13 -> x0, matrix products: 106 us -> none  [the longest x2 46.3 us: mlp_partial(): return jnp.dot(hidden_act, w_down, preferred_element_type=jnp.float32)]
    pallas_call x0 -> x2, Pallas kernels: none -> 97.6 us  [the longest x1 84.8 us: local_step(): pl.pallas_call(back_kernel, out_shape=jax.ShapeDtypeStruct((ROWS, WIDTH),...]
    pmax x1 -> x0, blocking collectives: 21.6 us -> none  [combine_sp(): glob_max = lax.pmax(part_max, 'sp')]
    psum x1 -> x0, blocking collectives: 16.9 us -> none  [combine_sp(): total_sum = lax.psum(part_sum * factor, 'sp')]
    select_n x2 -> x0, other arithmetic: 6.72 us -> none  [the longest x1 6.7 us: local_step(): k_new_cache = jnp.where(hit_mask, key_new[:, None], k_self)]
    reduce_sum x6 -> x0, other arithmetic: 6.35 us -> none  [the longest x5 5.91 us: rms_norm(): jnp.mean(vals32 * vals32, axis=-1, keepdims=True) + NORM_EPS]
    sub x1 -> x0, matrix products: 5.9 us -> none  [local_softmax(): scores - part_max[..., None]]
  transfers between devices with their start and end apart: 5 -> 0, of which waited for: 5 -> 0; matrix products, arithmetic and copies ran while one was open for 1% -> 0% of each run, Pallas kernels for 0% -> 0%
where the time goes in v1:
time: 100 us
  Pallas kernels  97.6 us (98%)
  local copies, waits for them, and re-layouts  1.87 us (2%)
    pallas_call x1, Pallas kernels, local_step(): pl.pallas_call(back_kernel, out_shape=jax.ShapeDtypeStruct((ROWS, WIDTH),...  84.8 us
    pallas_call x1, Pallas kernels, local_step(): pl.pallas_call(front_kernel, out_shape=(*[jax.ShapeDtypeStruct((ROWS, HD,...  12.8 us

profile of v1, /device:TPU:0, one launch (start us, length us, event | category | flops | bytes accessed | tf_op | source)
XLA Modules:
  0.0 100.1 jit_solution(16250371851184273988)
XLA Ops:
  0.6 12.8 %front.1 = (bf16[64,128,128]{2,1,0:T(8,128)(2,1)}, bf16[64,128,128]{2,1,0:T(8,128)(2,1)}, f32[512,128]{1,0:T(8,128)}, f32[64,128]{1,0:T(8,128)}) custom-call(s32[64]{0:T(128)} %pos_ref.1, bf16[64,4096]{1,0:T(8,128)(2,1)} %hid_hbm.3, bf16[32,128]{1,0:T(8,128)(2,1)} %bitcast.15, f32[1,128]{1,0:T(1,128)} %constant.2.clone.freq_ref, bf16[4096,1024]{1,0:T(8,128)(2,1)} %wq.1, ...), custom_call_target="tpu_custom_call" | custom-call | tf_op jit(solution)/shard_map/front/pallas_call | solution.py:601
  13.4 84.8 %back.1 = bf16[64,4096]{1,0:T(8,128)(2,1)} custom-call(s32[64]{0:T(128)} %mask_ref.1, f32[2]{0:T(128)} %gates_ref.1, f32[512,128]{1,0:T(8,128)} %get-tuple-element.7.o_part, f32[64,128]{1,0:T(8,128)} %get-tuple-element.8.stats, bf16[64,4096]{1,0:T(8,128)(2,1)} %hid_hbm.3, s32[64,256]{1,0:T(8,128)} %xv_hbm.1, bf16[32,128]{1,0:T(8,128)(2,1)} %bitcast.16, ...), custom_call_target="tpu_custom_call" | custom-call | tf_op jit(solution)/shard_map/back/pallas_call | solution.py:618
  98.2 1.9 %copy.31 = bf16[64,4096]{1,0:T(8,128)(2,1)} copy(bf16[64,4096]{1,0:T(8,128)(2,1)} %back.1) | data formatting | bytes 1048576

commit v2 on v1

v2 whole, which is shorter than its diff:
```python
import math
import numpy as np
import jax
import jax.numpy as jnp
from jax import lax
from jax.experimental import pallas as pl
from jax.experimental.pallas import tpu as pltpu
from jax.sharding import PartitionSpec as P

NORM_EPS = 1e-5
ROPE_THETA = 500000.0
ROPE_FACTOR = 8.0
LOW_FREQ = 1.0
HIGH_FREQ = 4.0
ORIG_CTX = 8192.0
NEG_BIG = -1e30
F32 = jnp.float32
BF16 = jnp.bfloat16
MESH_ID = pl.DeviceIdType.MESH

CW = 256
HD = 128
NH = 8
NQ = 4
ROWS = 64
NSP = 4
RB = 16
TBLK = 64
WIDTH = 4096
UNROLL = 8
VMEM_ALL = 67043328
NCH = 16
FF = 3584
QW = 1024
LAST = 3
NG = 8
SP_ORDER = (2, 1, 0)
BLK3 = (RB, NH, HD)
NPAIR = 12
SEG_QKV = (0, 3)
SEG_WO = (3, 2)
SEG_GU = (5, 14)
SEG_DN = (19, 8)
SEG_CQ = (27, 2)
SEG_CWO = (29, 2)
SEG_CGU = (31, 14)
SEG_CDN = (45, 8)


def rope_freqs(head_dim):
    f32 = np.float32
    inv_freq = (1.0 / (f32(ROPE_THETA) ** (np.arange(0, head_dim, 2).astype(f32) / f32(head_dim)))).astype(f32)
    wavelen = 2.0 * math.pi / inv_freq
    smooth = (ORIG_CTX / wavelen - LOW_FREQ) / (HIGH_FREQ - LOW_FREQ)
    mid_freq = (1.0 - smooth) * inv_freq / ROPE_FACTOR + smooth * inv_freq
    scaled = np.where(wavelen > ORIG_CTX / LOW_FREQ, inv_freq / ROPE_FACTOR, mid_freq)
    return np.where(wavelen < ORIG_CTX / HIGH_FREQ, inv_freq, scaled).astype(f32)


def blk(i, n):
    return pl.ds(pl.multiple_of(i * n, n), n)


def half_of(n, core):
    return pl.ds(n * 4 + 2 * core, 2)


def round_bf16(x):
    return x.astype(BF16).astype(F32)


def attend(queries, keys, values, limits, scale):
    scores = [lax.dot_general(q, k, (((1,), (1,)), ((), ())), preferred_element_type=F32)
              for q, k in zip(queries, keys)]
    lane = lax.broadcasted_iota(jnp.int32, scores[0].shape, 1)
    head = lax.broadcasted_iota(jnp.int32, scores[0].shape, 0)
    own = (lane & 1) == (head >> 2)
    slot = lane >> 1
    oks = [own & (slot < limit) for limit in limits]
    scores = [jnp.where(ok, sc * scale, NEG_BIG) for ok, sc in zip(oks, scores)]
    maxes = [jnp.max(sc, axis=1, keepdims=True) for sc in scores]
    probs = [jnp.where(ok, jnp.exp(sc - m), 0.0) for ok, sc, m in zip(oks, scores, maxes)]
    sums = [jnp.sum(p, axis=1, keepdims=True) for p in probs]
    outs = [jnp.dot(p.astype(BF16), v, preferred_element_type=F32) for p, v in zip(probs, values)]
    return maxes, sums, outs


def with_new(rows, pair, lp):
    row_t = lax.broadcasted_iota(jnp.int32, (HD, HD), 0)
    both = jnp.where((row_t & 1) == 0, pair[0:1, :], pair[1:2, :])
    return jnp.where((row_t >> 1) == lp, both, rows.astype(F32)).astype(BF16)


def step_kernel(pos_ref, mask_ref, gates_ref, hid_hbm, xv_hbm, g1_ref, g2_ref, g3_ref, g4_ref, qn_ref, freq_ref,
                k_hbm, v_hbm, wq, wk, wv, wo, wg, wu, wd, cq, cwo, cg, cu, cd, kc_hbm, vc_hbm,
                full, fresh,
                ring, kbuf, vbuf, hid, x, tab, cosb, sinb, qself, o_part, stats,
                xvb, cnt, gab, gmb, gsc, hres, xb, ab, ofl, osc, qsc, ro, rst, pb, r1, sb, r2, tb, l1, lsum, l2,
                rsem, csem, hsem, xsem, ksem, vsem, osem, stsem, a1s, a1r, a2s, a2r, a3s, a3r,
                b1s, b1r, b2s, b2r, os_, or_, zss, zrs, yss, yrs, dss, drs):
    s = lax.axis_index('sp')
    t = lax.axis_index('tp')
    c = lax.rem(t, 2)
    y = lax.div(t, 2)
    core_peer = {'tp': t + 1 - 2 * c}
    y_peer = {'tp': lax.rem(t + 2, 4)}
    sp_peers = [lax.rem(s + k, 4) for k in (1, 2, 3)]
    sp_from = [lax.rem(s + 4 - k, 4) for k in (1, 2, 3)]

    def cols(w, j):
        return w.at[:, blk(j, CW)]

    def tall(w, slot, sub, j):
        return [(cols(w, j), ring.at[slot, sub, pl.ds(0, w.shape[0])])]

    def square(w, slot, sub, j):
        rows = w.shape[0]
        return [(cols(w, 4 * j + k), ring.at[slot, sub, pl.ds(k * rows, rows)]) for k in range(4)]

    segments = (
        (SEG_WO, lambda sl, p: square(wo, sl, 0, 2 * p), lambda sl, p: square(wo, sl, 1, 2 * p + 1)),
        (SEG_GU, lambda sl, p: tall(wg, sl, 0, p), lambda sl, p: tall(wu, sl, 1, p)),
        (SEG_DN, lambda sl, p: tall(wd, sl, 0, 2 * p), lambda sl, p: tall(wd, sl, 1, 2 * p + 1)),
        (SEG_CQ, lambda sl, p: tall(cq, sl, 0, 2 * p), lambda sl, p: tall(cq, sl, 1, 2 * p + 1)),
        (SEG_CWO, lambda sl, p: square(cwo, sl, 0, 2 * p), lambda sl, p: square(cwo, sl, 1, 2 * p + 1)),
        (SEG_CGU, lambda sl, p: tall(cg, sl, 0, p), lambda sl, p: tall(cu, sl, 1, p)),
        (SEG_CDN, lambda sl, p: tall(cd, sl, 0, 2 * p), lambda sl, p: tall(cd, sl, 1, 2 * p + 1)),
    )

    def issue(pair, low, high):
        slot = lax.rem(pair, NPAIR)
        for (first, count), even, odd in segments:
            if first >= high or first + count <= low:
                continue

            def go(first=first, even=even, odd=odd):
                for sub, make in ((0, even), (1, odd)):
                    for src, dst in make(slot, pair - first):
                        pltpu.make_async_copy(src, dst, rsem.at[slot, sub]).start(priority=1)

            if first <= low and high <= first + count:
                go()
            else:
                pl.when((pair >= first) & (pair < first + count))(go)

    def arrive(slot, sub, rows):
        dst = ring.at[slot, sub, pl.ds(0, rows)]
        pltpu.make_async_copy(dst, dst, rsem.at[slot, sub]).wait()

    def send1(ar, n):
        return pltpu.make_async_remote_copy(
            pb.at[ar, half_of(n, 1 - c)], r1.at[ar, n], a1s, a1r.at[n],
            device_id=core_peer, device_id_type=MESH_ID)

    def send2(ar, n):
        return pltpu.make_async_remote_copy(
            sb.at[ar, n], r2.at[ar, n], a2s, a2r.at[ar % 2, n],
            device_id=y_peer, device_id_type=MESH_ID)

    def send3(ar, n):
        mine = tb.at[ar, half_of(n, c)]
        return pltpu.make_async_remote_copy(
            mine, mine, a3s, a3r.at[n], device_id=core_peer, device_id_type=MESH_ID)

    def stage2(ar, n):
        send1(ar, n).wait_recv()
        sb[ar, n] = pb[ar, half_of(n, c)] + r1[ar, n]
        send2(ar, n).start()

    def stage3(ar, n):
        send2(ar, n).wait_recv()
        tb[ar, half_of(n, c)] = sb[ar, n] + r2[ar, n]
        send3(ar, n).start()

    def drain(ar):
        stage3(ar, 2)
        stage3(ar, 3)
        for n in range(4):
            send3(ar, n).wait_recv()
        sent(pb.at[ar, pl.ds(0, NH)], a1s)
        sent(pb.at[ar, pl.ds(0, NH)], a2s)
        sent(pb.at[ar, pl.ds(0, NH)], a3s)

    def sent(ref, sem):
        pltpu.make_async_copy(ref, ref, sem).wait()

    def norm(g_ref, update):
        gsc[...] = g_ref[...].astype(F32)

        def add(q, acc):
            v = update(q)
            hres[q] = v
            return acc + v * v

        acc = lax.fori_loop(0, NCH, add, jnp.zeros((RB, CW), F32), unroll=4)
        inv = lax.rsqrt(jnp.sum(acc, axis=-1, keepdims=True) * (1.0 / WIDTH) + NORM_EPS)

        def put(q, carry):
            for u in range(2):
                cs = slice(u * HD, (u + 1) * HD)
                v = hres[q][:, cs] * inv * gsc[pl.ds(2 * q + u, 1), :]
                xb[:, pl.ds(pl.multiple_of(q * CW + u * HD, HD), HD)] = v.astype(BF16)
            return carry

        lax.fori_loop(0, NCH, put, 0, unroll=4)

    def project_out(ar, seg):
        first = seg[0]

        def pair(p, carry):
            slot = lax.rem(first + p, NPAIR)
            for sub in range(2):
                n = 2 * p + sub
                arrive(slot, sub, WIDTH)
                ps = [jnp.dot(ofl[...], ring[slot, sub, k * QW:(k + 1) * QW, :], preferred_element_type=F32)
                      for k in range(4)]
                for k in range(4):
                    pb[ar, n * 4 + k] = ps[k]
                send1(ar, n).start()
            issue(first + p + NPAIR, first + NPAIR, first + NPAIR + 2)
            return carry

        lax.fori_loop(0, 2, pair, 0)
        for n in range(3):
            stage2(ar, n)
        stage2(ar, 3)
        stage3(ar, 0)
        stage3(ar, 1)
        drain(ar)

    def gate_up(seg):
        first = seg[0]

        def two(p, carry):
            pairs = [2 * p, 2 * p + 1]
            slots = [lax.rem(first + j, NPAIR) for j in pairs]
            for slot in slots:
                for sub in range(2):
                    arrive(slot, sub, WIDTH)
            prods = [[jnp.dot(xb[...], ring[slot, sub], preferred_element_type=F32) for sub in range(2)]
                     for slot in slots]
            for j, (gate, up) in zip(pairs, prods):
                gate, up = round_bf16(gate), round_bf16(up)
                ab[:, blk(j, CW)] = (gate * jax.nn.sigmoid(gate) * up).astype(BF16)
            for j in pairs:
                issue(first + j + NPAIR, first + NPAIR, first + NPAIR + seg[1])
            return carry

        lax.fori_loop(0, seg[1] // 2, two, 0)

    def down_dots(idx):
        slots = [lax.rem(j, NPAIR) for j in idx]
        for slot in slots:
            for sub in range(2):
                arrive(slot, sub, FF)
        return [jnp.dot(ab[...], ring[slot, sub, :FF, :], preferred_element_type=F32)
                for slot in slots for sub in range(2)]

    def down(ar, seg):
        first = seg[0]

        def group(n, carry):
            idx = [first + 2 * n, first + 2 * n + 1]
            for k, part in enumerate(down_dots(idx)):
                pb[ar, n * 4 + k] = part
            for j in idx:
                issue(j + NPAIR, first + NPAIR, first + NPAIR + seg[1])
            send1(ar, n).start()

            @pl.when(n >= 1)
            def _():
                stage2(ar, n - 1)

            @pl.when(n >= 2)
            def _():
                stage3(ar, n - 2)

            return carry

        lax.fori_loop(0, 4, group, 0)
        stage2(ar, 3)
        drain(ar)

    def last1(n):
        return pltpu.make_async_remote_copy(
            pb.at[LAST, 2 * n + 1 - c], l1.at[n], b1s, b1r.at[n], device_id=core_peer, device_id_type=MESH_ID)

    def last2(n):
        return pltpu.make_async_remote_copy(
            lsum.at[n], l2.at[n], b2s, b2r.at[n], device_id=y_peer, device_id_type=MESH_ID)

    def own_core(n):
        mine = full.at[s, 2 * n + c]
        return pltpu.make_async_remote_copy(
            mine, mine, os_, or_, device_id=core_peer, device_id_type=MESH_ID)

    def strip(k, n, half):
        src = s if k is None else sp_from[k]
        return full.at[src, 2 * n + c, pl.ds(pl.multiple_of(half * NH, NH), NH)]

    def to_peer(piece, send, recv, peer):
        pltpu.make_async_remote_copy(
            piece, piece, send, recv, device_id=peer, device_id_type=MESH_ID).start()

    def last_stage2(n):
        last1(n).wait_recv()
        lsum[n] = pb[LAST, 2 * n + c] + l1[n]
        last2(n).start()

    def last_stage3(n, whole=False):
        last2(n).wait_recv()
        piece = 2 * n + c
        total = lsum[n] + l2[n]
        for w in range(2):
            cs = slice(w * HD, (w + 1) * HD)
            full[s, piece, :, cs] = round_bf16(hres[piece][:, cs] + gmb[...] * total[:, cs])
        own_core(n).start()
        for k in SP_ORDER:
            mine = full.at[s, piece] if whole else strip(None, n, y)
            to_peer(mine, zss, zrs.at[n], {'sp': sp_peers[k]})

    def z_arrive(n):
        sent(full.at[0, pl.ds(0, 3), pl.ds(0, NH)], zrs.at[n])
        for k in range(3):
            got = strip(k, n, y)
            to_peer(got, yss, yrs.at[n], y_peer)
            to_peer(got, dss, drs, core_peer)

    def y_arrive(n):
        sent(full.at[0, pl.ds(0, 3), pl.ds(0, NH)], yrs.at[n])
        for k in range(3):
            to_peer(strip(k, n, 1 - y), dss, drs, core_peer)

    def whole_arrive(n):
        sent(full.at[0, pl.ds(0, 3)], zrs.at[n])
        for k in range(3):
            to_peer(full.at[sp_from[k], 2 * n + c], dss, drs, core_peer)

    def down_last(seg):
        first = seg[0]

        def group(n, carry):
            for k, part in enumerate(down_dots([first + n])):
                pb[LAST, 2 * n + k] = part
            last1(n).start()

            @pl.when(n >= 1)
            def _():
                last_stage2(n - 1)

            @pl.when(n >= 3)
            def _():
                last_stage3(n - 3)

            return carry

        lax.fori_loop(0, NG, group, 0)
        last_stage2(NG - 1)

    def bytes_of(strips):
        if strips % 2 == 0 and strips <= 2 * NCH:
            return full.at[0, pl.ds(0, strips // 2)]
        return full.at[pl.ds(0, 3), pl.ds(0, strips // 3), pl.ds(0, NH)]

    def spread():
        last_stage3(5)
        z_arrive(0)
        last_stage3(6)
        z_arrive(1)
        last_stage3(7, whole=True)
        for n in range(2, 7):
            z_arrive(n)
            y_arrive(n - 2)
        y_arrive(5)
        whole_arrive(7)
        y_arrive(6)
        own = pl.ds(0, NG)
        for sem in (os_, or_, b1s, b2s):
            sent(full.at[0, own], sem)
        for sem, strips, pieces in ((zss, 21, 3), (yss, 21, 0), (dss, 42, 3), (drs, 42, 3)):
            sent(bytes_of(strips + 2 * pieces), sem)

    def heads_to_rows():
        for h in range(8):
            ofl[:, h * 128:(h + 1) * 128] = osc[pl.ds(h, 16, stride=8), :].astype(BF16)

    hcopy = pltpu.make_async_copy(hid_hbm, hid, hsem)
    hcopy.start()
    xcopy = pltpu.make_async_copy(xv_hbm.at[blk(s, RB)], xvb, xsem)
    xcopy.start()
    barrier = pltpu.get_barrier_semaphore()
    for peer in [core_peer, y_peer] + [{'sp': v} for v in sp_peers]:
        pl.semaphore_signal(barrier, inc=1, device_id=peer, device_id_type=MESH_ID)
    qkv_parts = [cols(wq, j) for j in range(NQ)] + [wk, wv]
    for j, part in enumerate(qkv_parts):
        pltpu.make_async_copy(part, ring.at[j // 2, j % 2], rsem.at[j // 2, j % 2]).start(priority=1)

    def block_of(i):
        return lax.rem(s + 3 - i, NSP)

    def cache_copies(i):
        j = block_of(i)
        return (pltpu.make_async_copy(k_hbm.at[blk(j, RB)], kbuf.at[blk(j, RB)], ksem.at[i]),
                pltpu.make_async_copy(v_hbm.at[blk(j, RB)], vbuf.at[blk(j, RB)], vsem.at[i]))

    for i in range(NSP):
        for cp in cache_copies(i):
            cp.start(priority=1)
    kcopy = pltpu.make_async_copy(kc_hbm.at[blk(s, ROWS)], kbuf, csem.at[0])
    vcopy = pltpu.make_async_copy(vc_hbm.at[blk(s, ROWS)], vbuf, csem.at[1])

    with jax.named_scope('tables'):
        gsc[...] = g1_ref[...].astype(F32)

        def fill(r, carry):
            tab[pl.ds(r, 1), :] = jnp.full((1, HD), pos_ref[r], jnp.int32).astype(F32)
            return carry

        lax.fori_loop(0, ROWS, fill, 0, unroll=8)
        angle = tab[...] * freq_ref[...]
        lanes = lax.broadcasted_iota(jnp.int32, (ROWS, HD), 1)
        sin_v = jnp.sin(angle)
        cosb[...] = jnp.cos(angle)
        sinb[...] = jnp.where(lanes < HD // 2, -sin_v, sin_v)
        for r in range(RB):
            gab[r:r + 1, :] = jnp.full((1, HD), mask_ref[s * RB + r], jnp.int32).astype(F32)
        on = gab[...]
        gab[...] = jnp.tanh(jnp.full((RB, HD), gates_ref[0], F32)) * on
        gmb[...] = jnp.tanh(jnp.full((RB, HD), gates_ref[1], F32)) * on
        xcopy.wait()
        cnt[...] = jnp.broadcast_to(jnp.sum((xvb[...] > 0).astype(jnp.int32), axis=1, keepdims=True), (RB, HD))

    with jax.named_scope('norm'):
        hcopy.wait()

        def norm_rows(r, carry):
            rows = blk(r, RB)
            acc = jnp.zeros((RB, HD), F32)
            for j in range(WIDTH // HD):
                v = hid[rows, j * HD:(j + 1) * HD].astype(F32)
                acc = acc + v * v
            inv = lax.rsqrt(jnp.sum(acc, axis=-1, keepdims=True) * (1.0 / WIDTH) + NORM_EPS)
            for j in range(WIDTH // HD):
                cs = slice(j * HD, (j + 1) * HD)
                x[rows, cs] = (hid[rows, cs].astype(F32) * inv * gsc[j:j + 1, :]).astype(BF16)
            return carry

        lax.fori_loop(0, NSP, norm_rows, 0)

    def rope(part):
        return round_bf16(part * cosb[...] + pltpu.roll(part, HD // 2, 1) * sinb[...])

    def qkv_pair(p):
        for sub in range(2):
            arrive(p, sub, WIDTH)
        return [round_bf16(jnp.dot(x[...], ring[p, sub], preferred_element_type=F32)) for sub in range(2)]

    with jax.named_scope('qkv'):
        def project(p, carry):
            for v, yv in enumerate(qkv_pair(p)):
                for u in range(2):
                    qself[pl.ds(4 * p + 2 * v + u, ROWS, stride=NH), :] = rope(yv[:, u * HD:(u + 1) * HD])
            issue(p + SEG_WO[0], SEG_WO[0], SEG_WO[0] + NQ // 2)
            return carry

        lax.fori_loop(0, NQ // 2, project, 0)
        last_pair = NQ // 2
        for v, yv in enumerate(qkv_pair(last_pair)):
            for u in range(2):
                part = yv[:, u * HD:(u + 1) * HD]
                fresh[pl.ds(2 * v + u, ROWS, stride=NH), :] = part if v else rope(part)
        for p in range(SEG_WO[0] + NQ // 2, SEG_WO[0] + NPAIR):
            issue(p, p, p + 1)

    lane8 = lax.broadcasted_iota(jnp.int32, (NH, HD), 1)
    head8 = lax.broadcasted_iota(jnp.int32, (NH, HD), 0)
    base = s * TBLK

    def part_copy(k):
        peer = lax.rem(s + k + 1, NSP)
        to = {'sp': peer}
        return (pltpu.make_async_remote_copy(o_part.at[blk(peer, HD)], ro.at[k], osem.at[0, k], osem.at[1, k],
                                             device_id=to, device_id_type=MESH_ID),
                pltpu.make_async_remote_copy(stats.at[blk(peer, RB)], rst.at[k], stsem.at[0, k], stsem.at[1, k],
                                             device_id=to, device_id_type=MESH_ID))

    def some_rows(rows):
        lps = [pos_ref[b] - base for b in rows]
        new = [fresh[blk(b, NH), :] for b in rows]
        queries = [qself[blk(b, NH), :].astype(BF16) for b in rows]
        keys = [with_new(kbuf[b], f[0:2], lp) for f, b, lp in zip(new, rows, lps)]
        values = [with_new(vbuf[b], f[2:4], lp) for f, b, lp in zip(new, rows, lps)]
        maxes, sums, outs = attend(queries, keys, values, [lp + 1 for lp in lps], HD ** -0.5)
        for b, m, l, o in zip(rows, maxes, sums, outs):
            o_part[blk(b, NH), :] = o
            st = jnp.where(lane8 == head8, m, 0.0) + jnp.where(lane8 == head8 + NH, l, 0.0)
            stats[pl.ds(b, 1), :] = jnp.sum(st, axis=0, keepdims=True)

    with jax.named_scope('bar'):
        pl.semaphore_wait(barrier, 5)
    with jax.named_scope('attend'):
        def block(i, carry):
            for cp in cache_copies(i):
                cp.wait()

            def some(g, carry2):
                some_rows([block_of(i) * RB + g * UNROLL + u for u in range(UNROLL)])
                return carry2

            lax.fori_loop(0, RB // UNROLL, some, 0)

            @pl.when(i < NSP - 1)
            def _():
                for cp in part_copy(NSP - 2 - i):
                    cp.start()

            return carry

        lax.fori_loop(0, NSP, block, 0)
        kcopy.start(priority=1)
        vcopy.start(priority=1)
    with jax.named_scope('parts'):
        for k in range(3):
            for cp in part_copy(k):
                cp.wait()

    lane3 = lax.broadcasted_iota(jnp.int32, BLK3, 2)
    head3 = lax.broadcasted_iota(jnp.int32, BLK3, 1)

    def pick(st, off):
        return jnp.sum(jnp.where(lane3 == head3 + off, st[:, None, :], 0.0), axis=2, keepdims=True)

    parts = [(o_part[blk(s, HD), :], stats[blk(s, RB), :])]
    parts += [(ro[k], rst[k]) for k in range(3)]
    maxes = [pick(st, 0) for _, st in parts]
    top = jnp.maximum(jnp.maximum(maxes[0], maxes[1]), jnp.maximum(maxes[2], maxes[3]))
    total = jnp.zeros(BLK3, F32)
    denom = jnp.zeros((16, 8, 1), F32)
    for (o, st), m in zip(parts, maxes):
        f = jnp.exp(m - top)
        denom = denom + pick(st, 8) * f
        total = total + o.reshape(BLK3) * f
    osc[...] = (total / denom).reshape(HD, HD)
    heads_to_rows()

    with jax.named_scope('wo'):
        project_out(0, SEG_WO)
    with jax.named_scope('norm2'):
        norm(g2_ref, lambda q: round_bf16(
            hid[blk(s, RB), blk(q, CW)].astype(F32) + tb[0, q]))
    with jax.named_scope('gu'):
        gate_up(SEG_GU)
    with jax.named_scope('dn'):
        down(1, SEG_DN)
    with jax.named_scope('norm3'):
        norm(g3_ref, lambda q: round_bf16(hres[q] + tb[1, q]))

    qn = qn_ref[...].astype(F32)
    first_q = SEG_CQ[0]
    with jax.named_scope('cq'):
        def queries(p, carry):
            slot = lax.rem(first_q + p, NPAIR)
            for sub in range(2):
                arrive(slot, sub, WIDTH)
            both = [jnp.dot(xb[...], ring[slot, sub], preferred_element_type=F32) for sub in range(2)]
            for sub in range(2):
                part = round_bf16(both[sub])
                for u in range(2):
                    v = part[:, u * HD:(u + 1) * HD]
                    inv = lax.rsqrt(jnp.mean(v * v, axis=-1, keepdims=True) + NORM_EPS)
                    qsc[pl.ds(4 * p + 2 * sub + u, RB, stride=NH), :] = round_bf16(v * inv * qn)
            issue(first_q + p + NPAIR, first_q + NPAIR, first_q + NPAIR + 2)
            return carry

        lax.fori_loop(0, 2, queries, 0)

    with jax.named_scope('cross'):
        kcopy.wait()
        vcopy.wait()

        def long_rows(buf, b):
            return buf[pl.ds(b * NSP, NSP)].reshape(NSP * HD, HD)

        def cross_rows(i, carry):
            bs = [i * 4 + u for u in range(4)]
            rows = [blk(b, NH) for b in bs]
            _, sums, outs = attend([qsc[r, :].astype(BF16) for r in rows], [long_rows(kbuf, b) for b in bs], [long_rows(vbuf, b) for b in bs],
                                   [cnt[pl.ds(b, 1), 0:1] for b in bs], HD ** -0.5)
            for r, l, o in zip(rows, sums, outs):
                osc[r, :] = o / l
            return carry

        lax.fori_loop(0, 4, cross_rows, 0)
        heads_to_rows()
    with jax.named_scope('cwo'):
        project_out(2, SEG_CWO)
    with jax.named_scope('norm4'):
        ga = jnp.concatenate([gab[...], gab[...]], axis=1)
        norm(g4_ref, lambda q: round_bf16(hres[q] + ga * tb[2, q]))
    with jax.named_scope('cgu'):
        gate_up(SEG_CGU)
    with jax.named_scope('cdn'):
        down_last(SEG_CDN)
    with jax.named_scope('spread'):
        spread()


def emit_kernel(pos_ref, full_hbm, fresh_hbm, k_hbm, v_hbm, out_hbm, k_out, v_out,
                full, fresh, kbuf, vbuf, out, fsem, nsem, ksem, vsem, kosem, vosem, osem):
    base = lax.axis_index('sp') * TBLK
    ncopy = pltpu.make_async_copy(fresh_hbm, fresh, nsem)
    ncopy.start()

    def copies(j):
        rows = blk(j, RB)
        return ((pltpu.make_async_copy(k_hbm.at[rows], kbuf.at[rows], ksem.at[j]),
                 pltpu.make_async_copy(v_hbm.at[rows], vbuf.at[rows], vsem.at[j])),
                (pltpu.make_async_copy(kbuf.at[rows], k_out.at[rows], kosem.at[j]),
                 pltpu.make_async_copy(vbuf.at[rows], v_out.at[rows], vosem.at[j])))

    for j in range(NSP):
        for cp in copies(j)[0]:
            cp.start()
    fcopy = pltpu.make_async_copy(full_hbm, full, fsem)
    fcopy.start()
    ncopy.wait()
    row_t = lax.broadcasted_iota(jnp.int32, (RB, HD), 0)

    def block(j, carry):
        ins, outs = copies(j)
        for cp in ins:
            cp.wait()

        def some(g, carry2):
            for u in range(UNROLL):
                b = j * RB + g * UNROLL + u
                new = fresh[blk(b, NH), :]
                lp = pos_ref[b] - base
                first = lax.div(jnp.clip(lp, 0, TBLK - 1), NH) * RB
                window = pl.ds(pl.multiple_of(first, RB), RB)
                for buf, pair in ((kbuf, new[0:2]), (vbuf, new[2:4])):
                    both = jnp.where((row_t & 1) == 0, pair[0:1, :], pair[1:2, :])
                    hit = (row_t >> 1) + lax.div(first, 2) == lp
                    buf[b, window, :] = jnp.where(hit, both, buf[b, window, :].astype(F32)).astype(BF16)
            return carry2

        lax.fori_loop(0, RB // UNROLL, some, 0)
        for cp in outs:
            cp.start()
        return carry

    lax.fori_loop(0, NSP, block, 0)
    fcopy.wait()

    def emit(q, carry):
        for r in range(NSP):
            out[r * RB:(r + 1) * RB, blk(q, CW)] = full[r, q].astype(BF16)
        return carry

    lax.fori_loop(0, NCH, emit, 0, unroll=4)
    ocopy = pltpu.make_async_copy(out, out_hbm, osem)
    ocopy.start()
    for j in range(NSP):
        for cp in copies(j)[1]:
            cp.wait()
    ocopy.wait()


def solution(mesh):
    cache_spec = P('dp', 'sp', 'tp', None)
    cross_spec = P('dp', None, 'tp', None)
    row_spec = P('dp', None)
    vec_spec = P('dp')
    full_spec = P(None)
    col_spec = P(None, 'tp')
    split_rows = P('tp', None)
    in_specs = (row_spec, vec_spec, cache_spec, cache_spec, cross_spec, cross_spec, row_spec, vec_spec,
                full_spec, col_spec, col_spec, col_spec, split_rows, full_spec, col_spec, col_spec, split_rows,
                full_spec, col_spec, full_spec, split_rows, full_spec, full_spec, col_spec, col_spec, split_rows)
    out_specs = (row_spec, cache_spec, cache_spec)
    vmem = pl.BlockSpec(memory_space=pltpu.VMEM)
    smem = pl.BlockSpec(memory_space=pltpu.SMEM)
    hbm = pl.BlockSpec(memory_space=pl.ANY)
    dma = pltpu.SemaphoreType.DMA

    def local_step(hidden, new_pos, k_self, v_self, k_cross, v_cross, xvalid, rowmask,
                   self_attn_norm, self_wq, self_wk, self_wv, self_wo, self_mlp_norm,
                   self_wgate, self_wup, self_wdown, cross_attn_norm, cross_wq, cross_qnorm,
                   cross_wo, cross_gates, cross_mlp_norm, cross_wgate, cross_wup, cross_wdown):
        half = rope_freqs(HD)
        freq = np.concatenate([half, half]).reshape(1, HD).astype(np.float32)

        def fold(gain):
            return gain.reshape(WIDTH // HD, HD)

        caches = [cache.reshape(ROWS, HD, HD) for cache in (k_self, v_self)]
        block_row = pltpu.VMEM((RB, HD), F32)
        table = pltpu.VMEM((ROWS, HD), F32)
        heads = pltpu.VMEM((ROWS * NH, HD), F32)
        cache_buf = pltpu.VMEM((ROWS, HD, HD), BF16)
        rows, fresh = pl.pallas_call(
            step_kernel,
            out_shape=(jax.ShapeDtypeStruct((NSP, NCH, RB, CW), F32), jax.ShapeDtypeStruct((ROWS * NH, HD), F32)),
            in_specs=[smem] * 3 + [hbm] * 2 + [vmem] * 6 + [hbm] * 16,
            out_specs=(vmem, vmem),
            scratch_shapes=[
                pltpu.VMEM((NPAIR, 2, WIDTH, CW), BF16),
                cache_buf, cache_buf,
                *[pltpu.VMEM((ROWS, WIDTH), BF16)] * 2, table, table, table, heads, heads, table,
                pltpu.VMEM((RB, 256), jnp.int32), pltpu.VMEM((RB, HD), jnp.int32), block_row, block_row,
                pltpu.VMEM((WIDTH // HD, HD), F32), pltpu.VMEM((NCH, RB, CW), F32),
                pltpu.VMEM((RB, WIDTH), BF16), pltpu.VMEM((RB, FF), BF16), pltpu.VMEM((RB, QW), BF16),
                *[pltpu.VMEM((HD, HD), F32)] * 2, pltpu.VMEM((3, HD, HD), F32), pltpu.VMEM((3, RB, HD), F32),
                pltpu.VMEM((4, NCH, RB, CW), F32), *[pltpu.VMEM((3, 4, 2, RB, CW), F32)] * 3,
                pltpu.VMEM((3, NCH, RB, CW), F32), *[pltpu.VMEM((NG, RB, CW), F32)] * 3,
                dma((NPAIR, 2)), dma((2,)), dma, dma, *[dma((NSP,))] * 2, *[dma((2, 3))] * 2, dma, dma((4,)), dma, dma((2, 4)), dma, dma((4,)),
                *[dma, dma((NG,))] * 2, dma, dma, *[dma, dma((NG,))] * 2, dma, dma],
            compiler_params=pltpu.CompilerParams(
                collective_id=0, has_side_effects=True, vmem_limit_bytes=VMEM_ALL),
            name='step',
        )(new_pos, rowmask, cross_gates, hidden, xvalid, fold(self_attn_norm), fold(self_mlp_norm),
          fold(cross_attn_norm), fold(cross_mlp_norm), cross_qnorm.reshape(1, -1), jnp.asarray(freq), *caches,
          self_wq, self_wk, self_wv, self_wo, self_wgate, self_wup, self_wdown,
          cross_wq, cross_wo, cross_wgate, cross_wup, cross_wdown,
          *[cache.reshape(-1, HD, HD) for cache in (k_cross, v_cross)])
        out, k_new, v_new = pl.pallas_call(
            emit_kernel,
            out_shape=(jax.ShapeDtypeStruct((ROWS, WIDTH), BF16), *[jax.ShapeDtypeStruct((ROWS, HD, HD), BF16)] * 2),
            in_specs=[smem] + [hbm] * 4, out_specs=(hbm,) * 3,
            scratch_shapes=[pltpu.VMEM((NSP, NCH, RB, CW), F32), heads, cache_buf, cache_buf,
                            pltpu.VMEM((ROWS, WIDTH), BF16), dma, dma, *[dma((NSP,))] * 4, dma],
            compiler_params=pltpu.CompilerParams(vmem_limit_bytes=VMEM_ALL),
            name='emit',
        )(new_pos, rows, fresh, *caches)
        return out, k_new.reshape(k_self.shape), v_new.reshape(v_self.shape)

    return jax.shard_map(local_step, mesh=mesh, in_specs=in_specs, out_specs=out_specs, check_vma=False)
```

time: 100 us -> 93.9 us (0.939)
  Pallas kernels: 97.6 us -> 93.1 us
  local copies, waits for them, and re-layouts: 1.87 us -> 0 us
    pallas_call x2, Pallas kernels: 97.6 us -> 93.1 us  [the longest x1 88 us: local_step(): pl.pallas_call(step_kernel, out_shape=(jax.ShapeDtypeStruct((NSP, NCH, RB...]
    unnamed x1 -> x0, local copies, waits for them, and re-layouts: 1.87 us -> none
where the time goes in v2:
time: 93.9 us; the launch traced here: 93.7 us
  Pallas kernels  93.1 us (99%)
    pallas_call x1, Pallas kernels, local_step(): pl.pallas_call(step_kernel, out_shape=(jax.ShapeDtypeStruct((NSP, NCH, RB...  88 us
    pallas_call x1, Pallas kernels, local_step(): pl.pallas_call(emit_kernel, out_shape=(jax.ShapeDtypeStruct((ROWS, WIDTH)...  5.02 us

profile of v2, /device:TPU:0, one launch (start us, length us, event | category | flops | bytes accessed | tf_op | source)
XLA Modules:
  0.0 93.7 jit_solution(12428584948678293156)
XLA Ops:
  0.6 88.0 %step.1 = (f32[4,16,16,256]{3,2,1,0:T(8,128)}, f32[512,128]{1,0:T(8,128)}) custom-call(s32[64]{0:T(128)} %pos_ref.3, s32[64]{0:T(128)} %mask_ref.1, f32[2]{0:T(128)} %gates_ref.1, bf16[64,4096]{1,0:T(8,128)(2,1)} %hid_hbm.1, s32[64,256]{1,0:T(8,128)} %xv_hbm.1, bf16[32,128]{1,0:T(8,128)(2,1)} %bitcast.17, bf16[32,128]{1,0:T(8,128)(2,1)} %bitcast.18, ...), custom_call_target="tpu_custom_call" | custom-call | tf_op jit(solution)/shard_map/step/pallas_call | solution.py:701
  88.7 5.0 %emit.1 = (bf16[64,4096]{1,0:T(8,128)(2,1)}, bf16[64,128,128]{2,1,0:T(8,128)(2,1)}, bf16[64,128,128]{2,1,0:T(8,128)(2,1)}) custom-call(s32[64]{0:T(128)} %pos_ref.3, f32[4,16,16,256]{3,2,1,0:T(8,128)} %get-tuple-element.8.full_hbm, f32[512,128]{1,0:T(8,128)} %get-tuple-element.9.fresh_hbm, bf16[64,128,128]{2,1,0:T(8,128)(2,1)} %bitcast.12, ...), custom_call_target="tpu_custom_call" | custom-call | tf_op jit(solution)/shard_map/emit/pallas_call | solution.py:726
